TPU v7x, 512 devices: a whole 4x8x8 slice. The times are simulated.
512 devices in a mesh: expert: 8 (over x, z_hi), tensor: 64 (over y, z_lo, core).
Axes of the slice: x: 4, y: 8, z: 8 (z_hi: 2, z_lo: 4; z = z_hi * 4 + z_lo), core: 2. Of those that a mesh axis runs over, the one named last changes fastest.
Arguments:
- tokens: bfloat16 [384, 6144], P('expert', 'tensor'), may hold values from -6 to 6
- expert_ids: int32 [384, 2], P('expert'), may hold values from 0 to 7, as said below
- route_weight: int32 [384, 2], P('expert'), may hold values from 1 to 4095
- gate_weight: bfloat16 [8, 6144, 8192], P('expert', None, 'tensor'), may hold values from -0.078125 to 0.078125
- up_weight: bfloat16 [8, 6144, 8192], P('expert', None, 'tensor'), may hold values from -0.078125 to 0.078125
- down_weight: bfloat16 [8, 8192, 6144], P('expert', 'tensor'), may hold values from -0.0625 to 0.0625
Outputs:
- mixed: bfloat16 [384, 6144], P('expert', 'tensor')
- expert_load: float32 [2, 8], replicated
Inputs may be any that keep to these rules, and one draw needn't show every extreme that they name: `expert_ids`: each row names two different experts. The hot expert is the one named in the first column of the first row of every aligned block of 48 rows (the tokens of one expert group), the same in all blocks. In each block exactly 42 rows name the hot expert, in either column; every other expert is named by 7 or 8 rows of each block, and by exactly 8 rows in some.
All inputs are finite; a program needn't handle non-finite values.
Results may differ from a plain program's by a relative error of at most 0.005.
Values may be sent and summed in bfloat16 or wider, within the bound.
A program may use at most 64 MiB of HBM per device.

v0:
```python
import jax
import jax.numpy as jnp
from jax import lax
from jax.sharding import PartitionSpec as P


def filled_up(lines, length):
    spare = -len(lines) % length
    return jnp.pad(lines, [(0, spare)] + [(0, 0)] * (lines.ndim - 1))


def from_root(value, axis, root):
    lines = jnp.where(lax.axis_index(axis) == root, value, jnp.zeros_like(value)).reshape(
        -1, *value.shape[1:][-1:]
    )
    padded = filled_up(lines, lax.axis_size(axis))
    own = lax.psum_scatter(padded, axis, scatter_dimension=0, tiled=True)
    return lax.all_gather(own, axis, axis=0, tiled=True)[: len(lines)].reshape(value.shape)


def gather_turned(arrays, axis, dims):
    turned = [jnp.moveaxis(a, dim, 0) for a, dim in zip(arrays, dims)]
    widths = [t[0].size for t in turned]
    both = jnp.concatenate([t.reshape(-1, w) for t, w in zip(turned, widths)], axis=1)
    out = lax.all_gather(both, axis, axis=0, tiled=True)
    blocks = jnp.split(out, [sum(widths[:k]) for k in range(1, len(widths))], axis=1)
    return tuple(
        (
            jnp.moveaxis(b.reshape(-1, *t.shape[1:]), 0, dim)
            for b, t, dim in zip(blocks, turned, dims)
        )
    )


def split_up(value, dim, length):
    lengths = value.shape
    blocks = value.reshape(*lengths[:dim], length, lengths[dim] // length, *lengths[dim + 1 :])
    return jnp.moveaxis(blocks, dim, 0)


def sum_at_owner(value, axis, dim):
    length = lax.axis_size(axis)
    blocks = lax.all_to_all(split_up(value, dim, length), axis, 0, 0, tiled=True)
    return jnp.sum(blocks, axis=0)


def from_everyone(value, axis):
    copies = jnp.broadcast_to(value, (lax.axis_size(axis), *value.shape))
    return lax.all_to_all(copies, axis, split_axis=0, concat_axis=0, tiled=True)


def of_everyone(value, axis):
    return from_everyone(value, axis).sum(axis=0)


def swiglu(gate_value, up_value):
    return (jax.nn.silu(gate_value) * up_value).astype(jnp.bfloat16)


def matmul(left, right):
    return jnp.dot(left, right, preferred_element_type=jnp.float32)


def route_stats(id_block, raw_block, labels):
    weights = raw_block.astype(jnp.float32)
    route_share = weights / jnp.sum(weights, axis=1, keepdims=True)
    flat_chosen = (
        (id_block[:, :, None] == labels[None, None, :])
        .astype(jnp.int32)
        .reshape(-1, labels.shape[0])
    )
    chosen_float = flat_chosen.astype(jnp.float32)
    stats = jnp.stack(
        [jnp.sum(chosen_float, axis=0), jnp.sum(route_share.reshape(-1, 1) * chosen_float, axis=0)]
    )
    return (route_share, flat_chosen, stats)


def local(tokens, expert_ids, route_weight, gate_weight, up_weight, down_weight):
    tok_rows = expert_ids.shape[0]
    experts = lax.axis_size("expert") * gate_weight.shape[0]
    hot_rows = tok_rows - tok_rows // 8 * min(experts - 2, 1)
    capacity = (2 * tok_rows - hot_rows + experts - 2) // (experts - 1)
    hot_id = expert_ids[0, 0]
    own_gate = gate_weight[0]
    own_up = up_weight[0]
    own_down = down_weight[0]
    hot_gate_w, hot_up_w, hot_down_w = (
        from_root(own_gate, "expert", hot_id),
        from_root(own_up, "expert", hot_id),
        from_root(own_down, "expert", hot_id),
    )
    labels = jnp.arange(experts, dtype=jnp.int32)
    route_share, flat_chosen, local_stats = route_stats(expert_ids, route_weight, labels)
    cold_chosen = flat_chosen * (labels != hot_id).astype(jnp.int32)[None, :]
    slot_index = jnp.sum((jnp.cumsum(cold_chosen, axis=0) - 1) * cold_chosen, axis=1)
    is_live = jnp.sum(cold_chosen, axis=1)
    target = jnp.sum(cold_chosen * labels[None, :], axis=1) * capacity + slot_index
    buffer_rows = jnp.arange(experts * capacity, dtype=jnp.int32)
    cold_pick = ((target[None, :] == buffer_rows[:, None]) & (is_live[None, :] == 1)).astype(
        jnp.bfloat16
    )
    cold_pick = jnp.sum(cold_pick.reshape(experts * capacity, tok_rows, 2), axis=2)
    hot_match = (expert_ids == hot_id).astype(jnp.int32)
    hot_flag = jnp.sum(hot_match, axis=1)
    hot_rank = jnp.cumsum(hot_flag) - 1
    hot_slots = jnp.arange(hot_rows, dtype=jnp.int32)
    hot_pick = ((hot_rank[None, :] == hot_slots[:, None]) & (hot_flag[None, :] == 1)).astype(
        jnp.bfloat16
    )
    feature_width = tokens.shape[1]
    cold_send = (
        matmul(cold_pick, tokens).astype(jnp.bfloat16).reshape(experts, capacity, feature_width)
    )
    cold_recv = lax.all_to_all(
        cold_send, "expert", split_axis=0, concat_axis=0, tiled=True
    ).reshape(experts * capacity, feature_width)
    hot_input = matmul(hot_pick, tokens).astype(jnp.bfloat16)
    cold_piece, hot_piece = gather_turned((cold_recv, hot_input), "tensor", (1, 1))
    cold_gate = matmul(cold_piece, own_gate)
    cold_up = matmul(cold_piece, own_up)
    hot_gate = matmul(hot_piece, hot_gate_w)
    hot_up = matmul(hot_piece, hot_up_w)
    cold_part = matmul(swiglu(cold_gate, cold_up), own_down)
    hot_part = matmul(swiglu(hot_gate, hot_up), hot_down_w)
    model_width = cold_part.shape[1]
    returned = lax.all_to_all(
        cold_part.reshape(experts, capacity, model_width),
        "expert",
        split_axis=0,
        concat_axis=0,
        tiled=True,
    ).reshape(experts * capacity, model_width)
    assign_weight = route_share.reshape(2 * tok_rows) * is_live.astype(jnp.float32)
    cold_out = jnp.sum(
        (returned[target] * assign_weight[:, None]).reshape(tok_rows, 2, model_width), axis=1
    )
    hot_weight = jnp.sum(route_share * hot_match.astype(jnp.float32), axis=1)
    hot_out = hot_part[jnp.clip(hot_rank, 0, hot_rows - 1)] * hot_weight[:, None]
    mixed = sum_at_owner(cold_out + hot_out, "tensor", 1).astype(jnp.bfloat16)
    expert_load = of_everyone(local_stats, "expert") / tok_rows
    return (mixed, expert_load)


def solution(mesh):
    placed = (
        P("expert", "tensor"),
        P("expert", None),
        P("expert", None),
        P("expert", None, "tensor"),
        P("expert", None, "tensor"),
        P("expert", "tensor", None),
    )
    return jax.shard_map(
        local, mesh=mesh, in_specs=placed, out_specs=(P("expert", "tensor"), P()), check_vma=False
    )
```

profile of v0, /device:TPU:1, one launch (start us, length us, event | category | flops | bytes accessed | tf_op | source)
XLA Modules:
  0.0 469.7 jit_solution(4374038837522308300)
XLA Ops:
  8.0 0.0 reduce-scatter.4.cloned.1.call-start
  8.1 1.2 slice.3
  9.9 2.7 bitcast_select_fusion.2
  12.6 0.0 reduce-scatter.8.cloned.1.call-start
  12.6 1.3 copy-done.4
  14.0 1.3 bitcast_select_fusion
  15.3 0.7 copy-done.6
  15.9 0.1 copy.58
  16.0 0.1 eq.79
  16.2 0.7 compare_convert_fusion.1
  16.8 0.1 fusion.42
  16.9 0.1 reduce_window_sum.18
  17.0 0.2 fusion.43
  17.3 0.1 add.79
  17.4 0.1 copy.59
  17.5 0.1 eq.88
  17.6 0.1 copy.60
  17.7 0.1 fusion.51
  17.8 0.8 fusion.28
  18.6 13.3 %all-to-all-start = ((bf16[8,8,96]{2,1,0:T(8,128)(2,1)}), bf16[8,8,96]{2,1,0:T(8,128)(2,1)S(1)}, u32[]{:S(2)}, u32[]{:S(2)}) async-start(bf16[8,8,96]{2,1,0:T(8,128)(2,1)} %fusion.28), calls=%async_computation | async-start | bytes 32768 | tf_op jit(solution)/shard_map/all_to_all | solution.py:115
  31.9 0.0 all-gather.5.cloned.1.call-start
  31.9 0.7 fusion.64
  32.6 0.1 copy.61
  32.7 0.1 reduce-window.4
  32.8 0.1 fusion.52
  32.9 0.1 fusion.34
  33.0 7.8 %all-to-all-done = bf16[8,8,96]{2,1,0:T(8,128)(2,1)S(1)} async-done(((bf16[8,8,96]{2,1,0:T(8,128)(2,1)}), bf16[8,8,96]{2,1,0:T(8,128)(2,1)S(1)}, u32[]{:S(2)}, u32[]{:S(2)}) %all-to-all-start) | async-done | bytes 12320 | tf_op jit(solution)/shard_map/all_to_all | solution.py:115
  40.9 0.7 copy.62
  41.6 0.0 reduce-scatter.6.cloned.1.call-start
  41.7 1.3 bitcast_select_fusion.1
  43.0 0.0 all-gather.7.cloned.1.call-start
  43.0 72.0 %reduce-scatter.4.cloned.1.call-done = bf16[768,128]{1,0:T(8,128)(2,1)} async-done(((bf16[6144,128]{1,0:T(8,128)(2,1)}), bf16[768,128]{1,0:T(8,128)(2,1)}) %reduce-scatter.4.cloned.1.call-update) | async-done | bytes 196624 | tf_op jit(solution)/shard_map/reduce_scatter | solution.py:17
  115.0 0.0 all-gather.11.cloned.1.call-start
  115.1 98.7 %reduce-scatter.8.cloned.1.call-done = bf16[16,6144]{1,0:T(8,128)(2,1)} async-done(((bf16[128,6144]{1,0:T(8,128)(2,1)}), bf16[16,6144]{1,0:T(8,128)(2,1)}) %reduce-scatter.8.cloned.1.call-update) | async-done | bytes 196624 | tf_op jit(solution)/shard_map/reduce_scatter | solution.py:17
  213.8 2.1 fusion.4
  215.9 4.0 fusion
  219.9 3.7 all-to-all-start.1
  223.7 0.0 all-gather.9.cloned.1.call-start
  223.7 107.7 %reduce-scatter.6.cloned.1.call-done = bf16[768,128]{1,0:T(8,128)(2,1)} async-done(((bf16[6144,128]{1,0:T(8,128)(2,1)}), bf16[768,128]{1,0:T(8,128)(2,1)}) %reduce-scatter.6.cloned.1.call-update) | async-done | bytes 196624 | tf_op jit(solution)/shard_map/reduce_scatter | solution.py:17
  331.5 0.1 convert_element_type.68
  331.6 0.1 copy.63
  331.7 0.7 multiply_reduce_fusion.4
  332.4 0.1 copy.66
  332.4 0.1 copy.64
  332.5 0.1 mul.107
  332.7 0.1 convert_reduce_fusion
  332.8 0.6 broadcast_in_dim.5
  333.4 3.6 all-to-all-start.3
  337.0 2.7 gather_fusion
  339.7 3.8 gather.11
  343.5 5.1 %multiply_reduce_fusion = f32[48,6144]{1,0:T(8,128)S(1)} fusion(f32[48,2,6144]{2,1,0:T(2,128)} %gather.11, f32[48,2]{1,0:T(8,128)S(1)} %copy.64), kind=kLoop, calls=%fused_computation.2 | loop fusion | flops 884736 | bytes 3539328 | tf_op jit(solution)/shard_map/reduce_sum | solution.py:135
  348.6 1.8 reduce_sum.120
  350.4 2.4 fusion.8
  352.8 0.0 all-gather.11.cloned.1.call-done
  352.9 49.2 %all-gather.9.cloned.1.call-done = bf16[6144,128]{1,0:T(8,128)(2,1)} async-done(((bf16[768,128]{1,0:T(8,128)(2,1)}), bf16[6144,128]{1,0:T(8,128)(2,1)}) %all-gather.9.cloned.1.call-update) | async-done | bytes 1572880 | tf_op jit(solution)/shard_map/all_gather | solution.py:18
  402.1 3.2 fusion.36
  405.3 1.9 gather_fusion.1
  407.3 2.0 gather.13
  409.3 0.2 add_bitcast_fusion
  409.5 2.1 copy.65
  411.6 10.4 %all-to-all-start.2 = ((f32[64,48,96]{2,1,0:T(8,128)}), f32[64,48,96]{2,1,0:T(8,128)S(1)}, u32[]{:S(2)}, u32[]{:S(2)}) async-start(f32[64,48,96]{2,1,0:T(8,128)} %copy.65), calls=%async_computation.5 | async-start | bytes 3145728 | tf_op jit(solution)/shard_map/all_to_all | solution.py:43
  422.0 0.6 broadcast_multiply_fusion
  422.5 39.1 %all-to-all-done.2 = f32[64,48,96]{2,1,0:T(8,128)S(1)} async-done(((f32[64,48,96]{2,1,0:T(8,128)}), f32[64,48,96]{2,1,0:T(8,128)S(1)}, u32[]{:S(2)}, u32[]{:S(2)}) %all-to-all-start.2) | async-done | bytes 1179680 | tf_op jit(solution)/shard_map/all_to_all | solution.py:43
  461.6 0.7 reduce_sum.122
  (36 shorter events, 0.3 us)
Async XLA Ops:
  8.0 9.8 %copy-start = (bf16[48,96]{1,0:T(8,128)(2,1)S(1)}, bf16[48,96]{1,0:T(8,128)(2,1)}, u32[]{:S(2)}) copy-start(bf16[48,96]{1,0:T(8,128)(2,1)} %param.6) | copy-start | bytes 27652
  8.0 107.0 %reduce-scatter.4.cloned.1.call-start = ((), (), s32[]{:S(2)}) async-start(), calls=%async_computation.8 | async-start | bytes 1769472 | tf_op jit(solution)/shard_map/reduce_scatter | solution.py:17
  12.6 1.4 copy-start.4
  12.6 201.1 %reduce-scatter.8.cloned.1.call-start = ((), (), s32[]{:S(2)}) async-start(), calls=%async_computation.12 | async-start | bytes 1769472 | tf_op jit(solution)/shard_map/reduce_scatter | solution.py:17
  15.3 0.7 copy-start.6
  15.3 26.4 %copy-start.5 = (bf16[1,6144,128]{2,1,0:T(8,128)(2,1)S(1)}, bf16[1,6144,128]{2,1,0:T(8,128)(2,1)}, u32[]{:S(2)}) copy-start(bf16[1,6144,128]{2,1,0:T(8,128)(2,1)} %param.10) | copy-start | bytes 4718596
  18.6 22.3 %all-to-all-start = ((bf16[8,8,96]{2,1,0:T(8,128)(2,1)}), bf16[8,8,96]{2,1,0:T(8,128)(2,1)S(1)}, u32[]{:S(2)}, u32[]{:S(2)}) async-start(bf16[8,8,96]{2,1,0:T(8,128)(2,1)} %fusion.28), calls=%async_computation | async-start | bytes 32768 | tf_op jit(solution)/shard_map/all_to_all | solution.py:115
  31.9 181.9 %all-gather.5.cloned.1.call-start = ((), (), s32[]{:S(2)}) async-start(), calls=%async_computation.7 | async-start | bytes 1597440 | tf_op jit(solution)/shard_map/all_gather | solution.py:25
  41.6 289.8 %reduce-scatter.6.cloned.1.call-start = ((), (), s32[]{:S(2)}) async-start(), calls=%async_computation.10 | async-start | bytes 1769472 | tf_op jit(solution)/shard_map/reduce_scatter | solution.py:17
  42.9 170.9 %copy-start.3 = (bf16[1,6144,128]{2,1,0:T(8,128)(2,1)S(1)}, bf16[1,6144,128]{2,1,0:T(8,128)(2,1)}, u32[]{:S(2)}) copy-start(bf16[1,6144,128]{2,1,0:T(8,128)(2,1)} %param.9) | copy-start | bytes 4718596
  43.0 307.5 %all-gather.7.cloned.1.call-start = ((), (), s32[]{:S(2)}) async-start(), calls=%async_computation.9 | async-start | bytes 1769472 | tf_op jit(solution)/shard_map/all_gather | solution.py:18
  115.0 237.9 %all-gather.11.cloned.1.call-start = ((), (), s32[]{:S(2)}) async-start(), calls=%async_computation.13 | async-start | bytes 1769472 | tf_op jit(solution)/shard_map/all_gather | solution.py:18
  213.8 2.1 copy-start.1
  219.9 111.7 %copy-start.7 = (s32[48,2]{0,1:T(2,128)S(1)}, s32[48,2]{0,1:T(2,128)}, u32[]{:S(2)}) copy-start(s32[48,2]{0,1:T(2,128)} %param.8) | copy-start | bytes 1156
  219.9 112.9 %all-to-all-start.1 = ((f32[8,8,6144]{2,1,0:T(8,128)}), f32[8,8,6144]{2,1,0:T(8,128)S(1)}, u32[]{:S(2)}, u32[]{:S(2)}) async-start(f32[8,8,6144]{2,1,0:T(8,128)} %fusion), calls=%async_computation.1 | async-start | bytes 3145728 | tf_op jit(solution)/shard_map/all_to_all | solution.py:127
  223.7 178.5 %all-gather.9.cloned.1.call-start = ((), (), s32[]{:S(2)}) async-start(), calls=%async_computation.11 | async-start | bytes 1769472 | tf_op jit(solution)/shard_map/all_gather | solution.py:18
  333.4 78.1 %all-to-all-start.3 = ((f32[8,2,8]{2,1,0:T(2,128)}), f32[8,2,8]{2,1,0:T(2,128)S(1)}, u32[]{:S(2)}, u32[]{:S(2)}) async-start(f32[8,2,8]{2,1,0:T(2,128)} %broadcast_in_dim.5), calls=%async_computation.6 | async-start | bytes 16384 | tf_op jit(solution)/shard_map/all_to_all | solution.py:49
  407.3 2.0 copy-start.2
  411.6 50.0 %all-to-all-start.2 = ((f32[64,48,96]{2,1,0:T(8,128)}), f32[64,48,96]{2,1,0:T(8,128)S(1)}, u32[]{:S(2)}, u32[]{:S(2)}) async-start(f32[64,48,96]{2,1,0:T(8,128)} %copy.65), calls=%async_computation.5 | async-start | bytes 3145728 | tf_op jit(solution)/shard_map/all_to_all | solution.py:43
Sparse Core Ops, SparseCore 0:
  13.4 101.5 reduce-scatter.3
  119.6 94.0 reduce-scatter.7
  218.4 113.0 reduce-scatter.5
Sparse Core Ops, SparseCore 1:
  41.7 119.9 all-gather.4
  164.7 75.4 all-gather.6
  243.3 80.9 all-gather.10
  331.5 70.5 all-gather.8
where the time goes:
time: 470 us
  waiting for transfers between devices  375 us (80%)
  starting transfers between devices  31.2 us (7%)
  local copies, waits for them, and re-layouts  20 us (4%)
  between operations  16.4 us (3%)
  other arithmetic  14.8 us (3%)
  matrix products  12.6 us (3%)
    reduce_scatter x3, waiting for transfers between devices, from_root(): own = lax.psum_scatter(padded, axis, scatter_dimension=0, tiled=True)  278 us
    all_gather x3, waiting for transfers between devices, from_root(): lax.all_gather(own, axis, axis=0, tiled=True)[:len(lines)]  49.3 us
    all_to_all x1, waiting for transfers between devices, sum_at_owner(): lax.all_to_all(split_up(value, dim, length), axis, 0, 0, tiled=True)  39.1 us
    all_to_all x1, starting transfers between devices, local(): lax.all_to_all(cold_send, 'expert', split_axis=0, concat_axis=0, tiled=True)  13.3 us
    dot_general x6, matrix products, matmul(): return jnp.dot(left, right, preferred_element_type=jnp.float32)  12.6 us
    all_to_all x1, starting transfers between devices, sum_at_owner(): lax.all_to_all(split_up(value, dim, length), axis, 0, 0, tiled=True)  10.4 us
  transfers between devices with their start and end apart: 11, of which 6 were waited for; matrix products, arithmetic and copies ran while one was open for 9% of the time, Pallas kernels for 0%

commit v1 on v0

v1 whole, which is shorter than its diff:
```python
import jax
import jax.numpy as jnp
from jax import lax
from jax.experimental import pallas as pl
from jax.experimental.pallas import tpu as pltpu
from jax.sharding import PartitionSpec as P

MESH = pl.DeviceIdType.MESH
F32 = jnp.float32
BF16 = jnp.bfloat16
RING = 8


def kernel(
    tok_ref, ids_ref, raw_ref, gate_ref, up_ref, down_ref,
    out_ref, load_ref,
    near, square, tabs, first, blocks, wk, dn, dk, acc, hid, scl,
    sent, came, own32, own16, direct, last_out, last_in,
    w_sem, d_sem, x_send, x_recv, t_send, t_recv, f_send, f_recv,
    a_send, a_recv, r_send, r_recv, l_send, l_recv, o_send, o_recv,
):
    e = lax.axis_index("expert")
    t = lax.axis_index("tensor")
    x, z_hi = e // 2, e % 2
    y, z_lo, c = t // 8, (t // 2) % 4, t % 2
    z = z_hi * 4 + z_lo
    half = x // 2
    p1 = z + c * (y - z)
    p2 = y + c * (z - y)

    def device(x_, y_, z_, c_):
        return (x_ * 2 + z_ // 4, (y_ * 4 + z_ % 4) * 2 + c_)

    def on_rings(a, b):
        return device(x, b + c * (a - b), a + c * (b - a), c)

    def remote(src, dst, send, recv, target):
        return pltpu.make_async_remote_copy(
            src_ref=src, dst_ref=dst, send_sem=send, recv_sem=recv,
            device_id=target, device_id_type=MESH,
        )

    sibling = device(x, y, z, 1 - c)

    def weight_rows(i, path):
        kb, j = i // 4, i % 4
        straight = kb * 768 + j * 192
        across = ((kb % 2) * 4 + j) * 768 + (kb // 2) * 192
        return pl.ds(pl.multiple_of(straight + path * (across - straight), 64), 192)

    def weight_slot(i, k):
        return wk.at[i // 4, pl.ds(pl.multiple_of((i % 4) * 192, 64), 192), pl.ds(pl.multiple_of(k * 128, 128), 128)]

    def local_weights(i, carry):
        rows = weight_rows(i, c)
        pltpu.make_async_copy(gate_ref.at[0, rows, :], weight_slot(i, c), w_sem.at[0]).start()
        pltpu.make_async_copy(up_ref.at[0, rows, :], weight_slot(i, 2 + c), w_sem.at[1]).start()
        return carry

    lax.fori_loop(0, 32, local_weights, 0)
    own_down = dn.at[pl.ds(pl.multiple_of(c * 128, 128), 128), :]
    their_down = dn.at[pl.ds(pl.multiple_of((1 - c) * 128, 128), 128), :]
    pltpu.make_async_copy(down_ref.at[0], own_down, d_sem.at[0]).start()

    barrier = pltpu.get_barrier_semaphore()

    def greet(target):
        pl.semaphore_signal(barrier, inc=1, device_id=target, device_id_type=MESH)

    for k in range(1, RING):
        other = (x * 2 + c + k) % 8
        greet(device(other // 2, y, z, other % 2))
        greet(on_rings((p1 + k) % RING, p2))
    for k in (1, 4, 7):
        greet(on_rings(p1, (p2 + k) % RING))

    lane = lax.broadcasted_iota(jnp.int32, (48, 128), 1)
    weights = raw_ref[...].astype(F32)
    share = weights / (weights[:, 0:1] + weights[:, 1:2])
    ids = ids_ref[...]
    hit0 = ids[:, 0:1] == lane
    hit1 = ids[:, 1:2] == lane
    zero = jnp.zeros((48, 128), F32)
    mix = jnp.where(hit0, share[:, 0:1], zero) + jnp.where(hit1, share[:, 1:2], zero)
    hits = jnp.where(hit0, 1.0, 0.0) + jnp.where(hit1, 1.0, 0.0)
    square[...] = jnp.zeros((128, 128), F32)
    square[0:48, :] = mix
    square[48:49, :] = jnp.sum(hits, axis=0, keepdims=True)
    square[49:50, :] = jnp.sum(mix, axis=0, keepdims=True)
    tabs[z_hi, x] = jnp.transpose(square[...])[0:8, :]

    pl.semaphore_wait(barrier, 17)

    for d in (2, 1, 3):
        remote(
            tok_ref, near.at[x % 2, c], x_send.at[d], x_recv.at[x % 2, c],
            device((x + d) % 4, y, z, half),
        ).start()

    @pl.when(half != c)
    def _():
        remote(tok_ref, near.at[x % 2, c], x_send.at[0], x_recv.at[x % 2, c], sibling).start()

    @pl.when(half == c)
    def _():
        near[x % 2, c] = tok_ref[...]

    table = lambda d: remote(
        tabs.at[z_hi, x], tabs.at[z_hi, x], t_send.at[d], t_recv.at[d],
        device((x + d) % 4, y, z, c),
    )
    for d in (1, 2, 3):
        table(d).start()

    def remote_weights(i, carry):
        rows = weight_rows(i, 1 - c)
        remote(gate_ref.at[0, rows, :], weight_slot(i, c), w_sem.at[2], w_sem.at[4], sibling).start()
        remote(up_ref.at[0, rows, :], weight_slot(i, 2 + c), w_sem.at[3], w_sem.at[5], sibling).start()
        return carry

    lax.fori_loop(0, 32, remote_weights, 0)
    down_copy = remote(down_ref.at[0], own_down, d_sem.at[1], d_sem.at[2], sibling)
    down_copy.start()

    for xh in range(2):
        for cs in range(2):
            @pl.when((2 * c + xh != x) | (c != cs))
            def _():
                remote(
                    tok_ref, near.at[xh, cs], x_send.at[0], x_recv.at[xh, cs], sibling
                ).wait_recv()

    pieces = [near[xh, cs].astype(F32) for xh in range(2) for cs in range(2)]
    first[p1] = jnp.concatenate(pieces, axis=1).astype(BF16)

    around = lambda k: remote(
        first.at[p1], first.at[p1], f_send.at[k], f_recv.at[k], on_rings((p1 + k) % RING, p2)
    )
    for k in (4, 3, 5, 2, 6, 1, 7):
        around(k).start()
    for d in (1, 2, 3):
        remote(
            tabs.at[z_hi, x], tabs.at[z_hi, (x + 4 - d) % 4], t_send.at[d], t_recv.at[d], sibling
        ).wait_recv()
    mirror = device(x, y, (z + 4) % 8, c)
    far_table = remote(tabs.at[z_hi], tabs.at[z_hi], t_send.at[0], t_recv.at[0], mirror)
    far_table.start()

    acc[...] = jnp.zeros_like(acc)
    for k in (1, 7, 2, 6, 3, 5, 4):
        remote(
            first.at[p1], first.at[(p1 + RING - k) % RING], f_send.at[k], f_recv.at[k], sibling
        ).wait_recv()

    def ring_copy(way, step, b, sub):
        target = on_rings(p1, (p2 + (1 if way == 0 else 7)) % RING)
        return remote(
            blocks.at[b, sub], blocks.at[b, sub],
            a_send.at[way, step, sub], a_recv.at[way, step, sub], target,
        )

    for h in range(2):
        for xh in range(2):
            sub = h * 2 + xh
            parts = [first[h * 4 + lo][:, xh * 192:(xh + 1) * 192].astype(F32) for lo in range(4)]
            blocks[p2, sub] = jnp.concatenate(parts, axis=1).astype(BF16)
            ring_copy(0, 0, p2, sub).start()
            ring_copy(1, 0, p2, sub).start()

    def place(b, h):
        across = (b % 4) * 2 + h
        return b + c * (across - b), h + c * (b // 4 - h)

    def project(b, h):
        kb, r = place(b, h)
        rows = blocks[b, pl.ds(2 * h, 2)].reshape(96, 768)
        acc[r] += jnp.dot(rows, wk[kb], preferred_element_type=F32)

    for k in range(2):
        mine = wk.at[:, :, pl.ds(pl.multiple_of((2 * k + c) * 128, 128), 128)]
        theirs = wk.at[:, :, pl.ds(pl.multiple_of((2 * k + 1 - c) * 128, 128), 128)]
        pltpu.make_async_copy(mine, mine, w_sem.at[k]).wait()
        pltpu.make_async_copy(theirs, theirs, w_sem.at[4 + k]).wait()
    project(p2, 0)
    project(p2, 1)
    pltpu.make_async_copy(down_ref.at[0], own_down, d_sem.at[0]).wait()
    pltpu.make_async_copy(down_ref.at[0], their_down, d_sem.at[2]).wait()

    @pl.when(c == 0)
    def _():
        for kb in range(8):
            dk[kb] = dn[:, kb * 768:(kb + 1) * 768]

    @pl.when(c == 1)
    def _():
        def repack(g, carry):
            rows = pl.ds(pl.multiple_of(g * 32, 32), 32)
            for kb in range(8):
                lo, hi = kb // 2, kb % 2
                cuts = [
                    dn[rows, (hi * 4 + j) * 768 + lo * 192:(hi * 4 + j) * 768 + (lo + 1) * 192].astype(F32)
                    for j in range(4)
                ]
                dk[kb, rows, :] = jnp.concatenate(cuts, axis=1).astype(BF16)
            return carry

        lax.fori_loop(0, 8, repack, 0)

    def gather_step(r, carry):
        held = ((p2 + RING - r) % RING, (p2 + r) % RING)
        for h in range(2):
            for xh in range(2):
                sub = h * 2 + xh
                for way in range(2):
                    ring_copy(way, r - 1, held[way], sub).wait_recv()
                    if h == way:
                        ring_copy(way, r, held[way], sub).start()
                    else:
                        @pl.when(r < 3)
                        def _():
                            ring_copy(way, r, held[way], sub).start()
            for way in range(2):
                project(held[way], h)
        return carry

    lax.fori_loop(1, 4, gather_step, 0)
    far = (p2 + 4) % RING
    for xh in range(2):
        for way in range(2):
            ring_copy(way, 3, far, way * 2 + xh).wait_recv()
    for way in range(2):
        project(far, way)

    remote(tabs.at[z_hi], tabs.at[1 - z_hi], t_send.at[0], t_recv.at[0], mirror).wait_recv()
    lane96 = lax.broadcasted_iota(jnp.int32, (128, 8), 1)
    for r in range(2):
        for xh in range(2):
            turned = jnp.transpose(tabs[r, 2 * c + xh])
            picked = jnp.sum(jnp.where(lane96 == e, turned, 0.0), axis=1, keepdims=True)
            scl[r, xh * 48:(xh + 1) * 48, :] = jnp.broadcast_to(picked[0:48], (48, 128))
        gate = acc[r, :, 0:256]
        up = acc[r, :, 256:512]
        hid[r] = (gate / (1.0 + jnp.exp(-gate)) * up).astype(BF16)
    everyone = tabs[0, 0]
    for k in range(1, 8):
        everyone = everyone + tabs[k // 4, k % 4]
    load_ref[...] = jnp.transpose(everyone)[48:50, :] / 48.0

    def own_part(q, h):
        kb, r = place(q, h)
        part = jnp.dot(hid[r], dk[kb], preferred_element_type=F32)
        return part * scl[r][:, 0:1]

    def sum_copy(way, s, sub):
        target = on_rings(p1, (p2 + (1 if way == 0 else 7)) % RING)
        return remote(
            sent.at[way, s, sub], came.at[way, s, sub],
            r_send.at[way, s, sub], r_recv.at[way, s, sub], target,
        )

    def pass_on(s, h, way, has_come):
        q = (p2 + (4 - s if way == 0 else 4 + s)) % RING
        part = own_part(q, h)
        for xh in range(2):
            sub = h * 2 + xh
            value = part[xh * 48:(xh + 1) * 48]
            if has_come:
                sum_copy(way, s - 1, sub).wait_recv()
                value = value + came[way, s - 1, sub].astype(F32)
            sent[way, s, sub] = value.astype(BF16)
            sum_copy(way, s, sub).start()

    for way in range(2):
        pass_on(0, way, way, False)
    for way in range(2):
        pass_on(1, 1 - way, way, False)
    for way in range(2):
        pass_on(1, way, way, True)

    def sum_step(s, carry):
        for way in range(2):
            pass_on(s, 1 - way, way, True)
        for way in range(2):
            pass_on(s, way, way, True)
        return carry

    lax.fori_loop(2, 4, sum_step, 0)

    scatter = lambda k: remote(
        own16.at[(p1 + k) % RING], direct.at[k], l_send.at[k], l_recv.at[k],
        on_rings((p1 + k) % RING, p2),
    )
    for h in range(2):
        part = own_part(p2, h)
        halves = []
        for xh in range(2):
            sub = h * 2 + xh
            value = part[xh * 48:(xh + 1) * 48]
            for way in range(2):
                sum_copy(way, 3, sub).wait_recv()
                value = value + came[way, 3, sub].astype(F32)
            halves.append(value)
        for lo in range(4):
            both = jnp.concatenate([v[:, lo * 192:(lo + 1) * 192] for v in halves], axis=1)
            own32[h * 4 + lo] = both
            own16[h * 4 + lo] = both.astype(BF16)
    for k in (4, 3, 5, 2, 6, 1, 7):
        scatter(k).start()
    total = own32[p1]
    for k in (1, 7, 2, 6, 3, 5, 4):
        scatter(k).wait_recv()
        total = total + direct[k].astype(F32)
    for xt in range(2):
        for ct in range(2):
            last_out[xt, ct] = total[:, xt * 192 + ct * 96:xt * 192 + (ct + 1) * 96]

    def home(xt, ct):
        return remote(
            last_out.at[xt, ct], last_in.at[x], o_send.at[xt, ct], o_recv.at[x],
            device(2 * c + xt, y, z, ct),
        )

    for xt in range(2):
        for ct in range(2):
            @pl.when((2 * c + xt != x) | (c != ct))
            def _():
                home(xt, ct).start()

    @pl.when(half == c)
    def _():
        last_in[x] = last_out[x % 2, c]

    for xs in range(4):
        @pl.when((xs != x) | (half != c))
        def _():
            remote(
                last_out.at[0, 0], last_in.at[xs], o_send.at[0, 0], o_recv.at[xs], sibling
            ).wait_recv()
    out_ref[...] = (last_in[0] + last_in[1] + last_in[2] + last_in[3]).astype(BF16)

    for xt in range(2):
        for ct in range(2):
            @pl.when((2 * c + xt != x) | (c != ct))
            def _():
                home(xt, ct).wait_send()
    for k in range(1, RING):
        scatter(k).wait_send()
        around(k).wait_send()
    for d in (1, 2, 3):
        table(d).wait_send()
        remote(
            tok_ref, near.at[x % 2, c], x_send.at[d], x_recv.at[x % 2, c],
            device((x + d) % 4, y, z, half),
        ).wait_send()

    @pl.when(half != c)
    def _():
        remote(tok_ref, near.at[x % 2, c], x_send.at[0], x_recv.at[x % 2, c], sibling).wait_send()

    far_table.wait_send()
    down_copy.wait_send()
    for k in range(2):
        mine = wk.at[:, :, pl.ds(pl.multiple_of((2 * k + c) * 128, 128), 128)]
        pltpu.make_async_copy(mine, mine, w_sem.at[2 + k]).wait()

    def left(s, carry):
        for way in range(2):
            for sub in range(4):
                ring_copy(way, s, p2, sub).wait_send()
                sum_copy(way, s + 1, sub).wait_send()
        return carry

    lax.fori_loop(0, 3, left, 0)
    for way in range(2):
        for xh in range(2):
            ring_copy(way, 3, p2, way * 2 + xh).wait_send()
            sum_copy(way, 0, way * 2 + xh).wait_send()


def local(tokens, expert_ids, route_weight, gate_weight, up_weight, down_weight):
    vmem, dma = pltpu.VMEM, pltpu.SemaphoreType.DMA
    inside = pl.BlockSpec(memory_space=pltpu.VMEM)
    outside = pl.BlockSpec(memory_space=pl.ANY)
    return pl.pallas_call(
        kernel,
        name="layer",
        out_shape=(
            jax.ShapeDtypeStruct((48, 96), BF16),
            jax.ShapeDtypeStruct((2, 8), F32),
        ),
        in_specs=[inside] * 3 + [outside] * 3,
        out_specs=(inside, inside),
        scratch_shapes=[
            vmem((2, 2, 48, 96), BF16),
            vmem((128, 128), F32),
            vmem((2, 4, 8, 128), F32),
            vmem((8, 48, 384), BF16),
            vmem((8, 4, 48, 768), BF16),
            vmem((8, 768, 512), BF16),
            vmem((256, 6144), BF16),
            vmem((8, 256, 768), BF16),
            vmem((2, 96, 512), F32),
            vmem((2, 96, 256), BF16),
            vmem((2, 96, 128), F32),
            vmem((2, 4, 4, 48, 768), BF16),
            vmem((2, 4, 4, 48, 768), BF16),
            vmem((8, 48, 384), F32),
            vmem((8, 48, 384), BF16),
            vmem((8, 48, 384), BF16),
            vmem((2, 2, 48, 96), F32),
            vmem((4, 48, 96), F32),
            dma((6,)),
            dma((3,)),
            dma((4,)),
            dma((2, 2)),
            dma((4,)),
            dma((4,)),
            dma((8,)),
            dma((8,)),
            dma((2, 4, 4)),
            dma((2, 4, 4)),
            dma((2, 4, 4)),
            dma((2, 4, 4)),
            dma((8,)),
            dma((8,)),
            dma((2, 2)),
            dma((4,)),
        ],
        compiler_params=pltpu.CompilerParams(
            collective_id=0, has_side_effects=True, vmem_limit_bytes=48 * 1024 * 1024
        ),
    )(tokens, expert_ids, route_weight, gate_weight, up_weight, down_weight)


def solution(mesh):
    placed = (
        P("expert", "tensor"),
        P("expert", None),
        P("expert", None),
        P("expert", None, "tensor"),
        P("expert", None, "tensor"),
        P("expert", "tensor", None),
    )
    return jax.shard_map(
        local, mesh=mesh, in_specs=placed, out_specs=(P("expert", "tensor"), P()), check_vma=False
    )
```

time: 470 us -> 85 us (0.18)
  waiting for transfers between devices: 375 us -> 0 us
  Pallas kernels: 0 us -> 76.4 us
  starting transfers between devices: 31.2 us -> 0 us
  between operations: 16.4 us -> 0.64 us
  other arithmetic: 14.8 us -> 0 us
  matrix products: 12.6 us -> 0 us
  local copies, waits for them, and re-layouts: 20 us -> 7.62 us
    reduce_scatter x3 -> x0, waiting for transfers between devices: 278 us -> none  [from_root(): own = lax.psum_scatter(padded, axis, scatter_dimension=0, tiled=True)]
    pallas_call x0 -> x1, Pallas kernels: none -> 76.4 us  [local(): pl.pallas_call(kernel, name='layer', out_shape=(jax.ShapeDtypeStruct((48,...]
    all_gather x4 -> x0, waiting for transfers between devices: 49.3 us -> none  [the longest x3 49.3 us: from_root(): lax.all_gather(own, axis, axis=0, tiled=True)[:len(lines)]]
    all_to_all x4 -> x0, waiting for transfers between devices: 46.9 us -> none  [the longest x1 39.1 us: sum_at_owner(): lax.all_to_all(split_up(value, dim, length), axis, 0, 0, tiled=True)]
    all_to_all x4 -> x0, starting transfers between devices: 30.9 us -> none  [the longest x1 13.3 us: local(): lax.all_to_all(cold_send, 'expert', split_axis=0, concat_axis=0, tiled=True)]
    dot_general x6 -> x0, matrix products: 12.6 us -> none  [matmul(): return jnp.dot(left, right, preferred_element_type=jnp.float32)]
    gather x4 -> x0, local copies, waits for them, and re-layouts: 10.4 us -> none  [the longest x2 6.5 us: local(): returned[target] * assign_weight[:, None]]
    reduce_sum x9 -> x0, other arithmetic: 7.66 us -> none  [the longest x1 5.09 us: local(): jnp.sum((returned[target] * assign_weight[:, None]).reshape(tok_rows, 2,...]
  transfers between devices with their start and end apart: 11 -> 0, of which waited for: 6 -> 0; matrix products, arithmetic and copies ran while one was open for 9% -> 0% of each run, Pallas kernels for 0% -> 0%
where the time goes in v1:
time: 85 us; the launch traced here: 84.7 us
  Pallas kernels  76.4 us (90%)
  local copies, waits for them, and re-layouts  7.62 us (9%)
    pallas_call x1, Pallas kernels, local(): pl.pallas_call(kernel, name='layer', out_shape=(jax.ShapeDtypeStruct((48,...  76.4 us
    unnamed x12, local copies, waits for them, and re-layouts  7.62 us

profile of v1, /device:TPU:1, one launch (start us, length us, event | category | flops | bytes accessed | tf_op | source)
XLA Modules:
  0.0 84.7 jit_solution(12129180823631039565)
XLA Ops:
  0.6 0.8 copy.8.ids_ref
  1.4 0.8 copy.9.raw_ref
  2.2 0.0 copy-start
  2.2 1.4 %copy-done = bf16[1,6144,128]{2,1,0:T(8,128)(2,1)S(1)} copy-done((bf16[1,6144,128]{2,1,0:T(8,128)(2,1)S(1)}, bf16[1,6144,128]{2,1,0:T(8,128)(2,1)}, u32[]{:S(2)}) %copy-start) | copy-done | bytes 1572888
  3.6 0.0 copy-start.1
  3.6 1.4 %copy-done.1 = bf16[1,6144,128]{2,1,0:T(8,128)(2,1)S(1)} copy-done((bf16[1,6144,128]{2,1,0:T(8,128)(2,1)S(1)}, bf16[1,6144,128]{2,1,0:T(8,128)(2,1)}, u32[]{:S(2)}) %copy-start.1) | copy-done | bytes 1572888
  5.0 0.0 copy-start.2
  5.0 1.4 %copy-done.2 = bf16[1,128,6144]{2,1,0:T(8,128)(2,1)S(1)} copy-done((bf16[1,128,6144]{2,1,0:T(8,128)(2,1)S(1)}, bf16[1,128,6144]{2,1,0:T(8,128)(2,1)}, u32[]{:S(2)}) %copy-start.2) | copy-done | bytes 1572888
  6.4 0.0 copy-start.3
  6.4 0.7 copy-done.3
  7.1 76.4 %layer.1 = (bf16[48,96]{1,0:T(8,128)(2,1)S(1)}, f32[2,8]{1,0:T(2,128)S(1)}) custom-call(bf16[48,96]{1,0:T(8,128)(2,1)S(1)} %copy-done.3, s32[48,2]{1,0:T(8,128)S(1)} %copy.8.ids_ref, s32[48,2]{1,0:T(8,128)S(1)} %copy.9.raw_ref, bf16[1,6144,128]{2,1,0:T(8,128)(2,1)S(1)} %copy-done, bf16[1,6144,128]{2,1,0:T(8,128)(2,1)S(1)} %copy-done.1, ...), custom_call_target="tpu_custom_call" | custom-call | tf_op jit(solution)/shard_map/layer/pallas_call | solution.py:384
  83.5 0.6 copy.12
  84.1 0.6 copy.13
Async XLA Ops:
  2.2 1.4 %copy-start = (bf16[1,6144,128]{2,1,0:T(8,128)(2,1)S(1)}, bf16[1,6144,128]{2,1,0:T(8,128)(2,1)}, u32[]{:S(2)}) copy-start(bf16[1,6144,128]{2,1,0:T(8,128)(2,1)} %gate_ref.1) | copy-start | bytes 4718596
  3.6 1.4 %copy-start.1 = (bf16[1,6144,128]{2,1,0:T(8,128)(2,1)S(1)}, bf16[1,6144,128]{2,1,0:T(8,128)(2,1)}, u32[]{:S(2)}) copy-start(bf16[1,6144,128]{2,1,0:T(8,128)(2,1)} %up_ref.1) | copy-start | bytes 4718596
  5.0 1.4 %copy-start.2 = (bf16[1,128,6144]{2,1,0:T(8,128)(2,1)S(1)}, bf16[1,128,6144]{2,1,0:T(8,128)(2,1)}, u32[]{:S(2)}) copy-start(bf16[1,128,6144]{2,1,0:T(8,128)(2,1)} %down_ref.1) | copy-start | bytes 4718596
  6.4 0.7 copy-start.3

commit v2 on v1

--- a/solution.py
+++ b/solution.py
@@ -12,12 +12,12 @@
 
 
 def kernel(
-    tok_ref, ids_ref, raw_ref, gate_ref, up_ref, down_ref,
+    tok_hbm, ids_hbm, raw_hbm, gate_ref, up_ref, down_ref,
     out_ref, load_ref,
-    near, square, tabs, first, blocks, wk, dn, dk, acc, hid, scl,
+    tok_ref, ids_ref, raw_ref, near, tabs, first, blocks, wk, dn, dk, acc, hid, scl, ahead,
     sent, came, own32, own16, direct, last_out, last_in,
-    w_sem, d_sem, x_send, x_recv, t_send, t_recv, f_send, f_recv,
-    a_send, a_recv, r_send, r_recv, l_send, l_recv, o_send, o_recv,
+    in_sem, w_sem, d_sem, x_send, x_recv, t_send, t_recv, f_send, f_recv,
+    a_send, a_recv, r_send, r_recv, l_send, l_recv, o_send, o_recv, pair_sem,
 ):
     e = lax.axis_index("expert")
     t = lax.axis_index("tensor")
@@ -42,26 +42,6 @@
 
     sibling = device(x, y, z, 1 - c)
 
-    def weight_rows(i, path):
-        kb, j = i // 4, i % 4
-        straight = kb * 768 + j * 192
-        across = ((kb % 2) * 4 + j) * 768 + (kb // 2) * 192
-        return pl.ds(pl.multiple_of(straight + path * (across - straight), 64), 192)
-
-    def weight_slot(i, k):
-        return wk.at[i // 4, pl.ds(pl.multiple_of((i % 4) * 192, 64), 192), pl.ds(pl.multiple_of(k * 128, 128), 128)]
-
-    def local_weights(i, carry):
-        rows = weight_rows(i, c)
-        pltpu.make_async_copy(gate_ref.at[0, rows, :], weight_slot(i, c), w_sem.at[0]).start()
-        pltpu.make_async_copy(up_ref.at[0, rows, :], weight_slot(i, 2 + c), w_sem.at[1]).start()
-        return carry
-
-    lax.fori_loop(0, 32, local_weights, 0)
-    own_down = dn.at[pl.ds(pl.multiple_of(c * 128, 128), 128), :]
-    their_down = dn.at[pl.ds(pl.multiple_of((1 - c) * 128, 128), 128), :]
-    pltpu.make_async_copy(down_ref.at[0], own_down, d_sem.at[0]).start()
-
     barrier = pltpu.get_barrier_semaphore()
 
     def greet(target):
@@ -74,21 +54,51 @@
     for k in (1, 4, 7):
         greet(on_rings(p1, (p2 + k) % RING))
 
-    lane = lax.broadcasted_iota(jnp.int32, (48, 128), 1)
+    def weight_rows(i, path):
+        kb, j = i // 4, i % 4
+        straight = kb * 768 + j * 192
+        across = ((kb % 2) * 4 + j) * 768 + (kb // 2) * 192
+        return pl.ds(pl.multiple_of(straight + path * (across - straight), 64), 192)
+
+    def weight_slot(i, k):
+        return wk.at[i // 4, pl.ds(pl.multiple_of((i % 4) * 192, 64), 192), pl.ds(pl.multiple_of(k * 128, 128), 128)]
+
+    def local_weights(i, carry):
+        rows = weight_rows(i, c)
+        pltpu.make_async_copy(gate_ref.at[0, rows, :], weight_slot(i, c), w_sem.at[0]).start()
+        pltpu.make_async_copy(up_ref.at[0, rows, :], weight_slot(i, 2 + c), w_sem.at[1]).start()
+        return carry
+
+    tok_copy = pltpu.make_async_copy(tok_hbm, tok_ref, in_sem.at[0])
+    ids_copy = pltpu.make_async_copy(ids_hbm, ids_ref, in_sem.at[1])
+    raw_copy = pltpu.make_async_copy(raw_hbm, raw_ref, in_sem.at[2])
+    tok_copy.start()
+    ids_copy.start()
+    raw_copy.start()
+    own_down = dn.at[pl.ds(pl.multiple_of(c * 128, 128), 128), :]
+    their_down = dn.at[pl.ds(pl.multiple_of((1 - c) * 128, 128), 128), :]
+    pltpu.make_async_copy(down_ref.at[0], own_down, d_sem.at[0]).start()
+
+    lax.fori_loop(0, 32, local_weights, 0)
+
+    ids_copy.wait()
+    raw_copy.wait()
+    row = lax.broadcasted_iota(jnp.int32, (8, 48), 0)
     weights = raw_ref[...].astype(F32)
-    share = weights / (weights[:, 0:1] + weights[:, 1:2])
+    share = weights / (weights[0:1, :] + weights[1:2, :])
     ids = ids_ref[...]
-    hit0 = ids[:, 0:1] == lane
-    hit1 = ids[:, 1:2] == lane
-    zero = jnp.zeros((48, 128), F32)
-    mix = jnp.where(hit0, share[:, 0:1], zero) + jnp.where(hit1, share[:, 1:2], zero)
-    hits = jnp.where(hit0, 1.0, 0.0) + jnp.where(hit1, 1.0, 0.0)
-    square[...] = jnp.zeros((128, 128), F32)
-    square[0:48, :] = mix
-    square[48:49, :] = jnp.sum(hits, axis=0, keepdims=True)
-    square[49:50, :] = jnp.sum(mix, axis=0, keepdims=True)
-    tabs[z_hi, x] = jnp.transpose(square[...])[0:8, :]
-
+    zero = jnp.zeros((8, 48), F32)
+    hit0 = ids[0:1, :] == row
+    hit1 = ids[1:2, :] == row
+    mix = jnp.where(hit0, share[0:1, :], zero) + jnp.where(hit1, share[1:2, :], zero)
+    hits = jnp.where(hit0, 1.0, zero) + jnp.where(hit1, 1.0, zero)
+    tabs[z_hi, x, :, 0:48] = mix
+    tabs[z_hi, x, :, 48:128] = jnp.where(
+        lax.broadcasted_iota(jnp.int32, (8, 80), 1) == 0,
+        jnp.sum(hits, axis=1, keepdims=True), jnp.sum(mix, axis=1, keepdims=True),
+    )
+
+    tok_copy.wait()
     pl.semaphore_wait(barrier, 17)
 
     for d in (2, 1, 3):
@@ -134,7 +144,7 @@
     first[p1] = jnp.concatenate(pieces, axis=1).astype(BF16)
 
     around = lambda k: remote(
-        first.at[p1], first.at[p1], f_send.at[k], f_recv.at[k], on_rings((p1 + k) % RING, p2)
+        first.at[p1], first.at[p1], f_send.at[0], f_recv.at[k], on_rings((p1 + k) % RING, p2)
     )
     for k in (4, 3, 5, 2, 6, 1, 7):
         around(k).start()
@@ -149,23 +159,27 @@
     acc[...] = jnp.zeros_like(acc)
     for k in (1, 7, 2, 6, 3, 5, 4):
         remote(
-            first.at[p1], first.at[(p1 + RING - k) % RING], f_send.at[k], f_recv.at[k], sibling
+            first.at[p1], first.at[(p1 + RING - k) % RING], f_send.at[0], f_recv.at[k], sibling
         ).wait_recv()
 
     def ring_copy(way, step, b, sub):
         target = on_rings(p1, (p2 + (1 if way == 0 else 7)) % RING)
         return remote(
             blocks.at[b, sub], blocks.at[b, sub],
-            a_send.at[way, step, sub], a_recv.at[way, step, sub], target,
+            a_send.at[0], a_recv.at[way, step, sub], target,
         )
 
     for h in range(2):
         for xh in range(2):
-            sub = h * 2 + xh
-            parts = [first[h * 4 + lo][:, xh * 192:(xh + 1) * 192].astype(F32) for lo in range(4)]
-            blocks[p2, sub] = jnp.concatenate(parts, axis=1).astype(BF16)
-            ring_copy(0, 0, p2, sub).start()
-            ring_copy(1, 0, p2, sub).start()
+            for lh in range(2):
+                sub = h * 4 + xh * 2 + lh
+                parts = [
+                    first[h * 4 + lh * 2 + lo][:, xh * 192:(xh + 1) * 192].astype(F32)
+                    for lo in range(2)
+                ]
+                blocks[p2, sub] = jnp.concatenate(parts, axis=1).astype(BF16)
+                ring_copy(0, 0, p2, sub).start()
+                ring_copy(1, 0, p2, sub).start()
 
     def place(b, h):
         across = (b % 4) * 2 + h
@@ -173,7 +187,10 @@
 
     def project(b, h):
         kb, r = place(b, h)
-        rows = blocks[b, pl.ds(2 * h, 2)].reshape(96, 768)
+        part = blocks[b, pl.ds(4 * h, 4)]
+        rows = jnp.concatenate(
+            [jnp.concatenate([part[2 * xh], part[2 * xh + 1]], axis=1) for xh in range(2)], axis=0
+        )
         acc[r] += jnp.dot(rows, wk[kb], preferred_element_type=F32)
 
     for k in range(2):
@@ -209,8 +226,7 @@
     def gather_step(r, carry):
         held = ((p2 + RING - r) % RING, (p2 + r) % RING)
         for h in range(2):
-            for xh in range(2):
-                sub = h * 2 + xh
+            for sub in range(h * 4, h * 4 + 4):
                 for way in range(2):
                     ring_copy(way, r - 1, held[way], sub).wait_recv()
                     if h == way:
@@ -225,9 +241,9 @@
 
     lax.fori_loop(1, 4, gather_step, 0)
     far = (p2 + 4) % RING
-    for xh in range(2):
+    for sub in range(4):
         for way in range(2):
-            ring_copy(way, 3, far, way * 2 + xh).wait_recv()
+            ring_copy(way, 3, far, way * 4 + sub).wait_recv()
     for way in range(2):
         project(far, way)
 
@@ -255,15 +271,18 @@
         target = on_rings(p1, (p2 + (1 if way == 0 else 7)) % RING)
         return remote(
             sent.at[way, s, sub], came.at[way, s, sub],
-            r_send.at[way, s, sub], r_recv.at[way, s, sub], target,
+            r_send.at[0], r_recv.at[way, s, sub], target,
         )
 
-    def pass_on(s, h, way, has_come):
+    def prepare(s, k, way):
         q = (p2 + (4 - s if way == 0 else 4 + s)) % RING
-        part = own_part(q, h)
+        ahead[way, k] = own_part(q, 1 - way if k == 0 else way)
+
+    def pass_on(s, k, way, has_come):
+        h = 1 - way if k == 0 else way
         for xh in range(2):
             sub = h * 2 + xh
-            value = part[xh * 48:(xh + 1) * 48]
+            value = ahead[way, k, xh * 48:(xh + 1) * 48, :]
             if has_come:
                 sum_copy(way, s - 1, sub).wait_recv()
                 value = value + came[way, s - 1, sub].astype(F32)
@@ -271,31 +290,42 @@
             sum_copy(way, s, sub).start()
 
     for way in range(2):
-        pass_on(0, way, way, False)
-    for way in range(2):
-        pass_on(1, 1 - way, way, False)
-    for way in range(2):
-        pass_on(1, way, way, True)
+        prepare(0, 1, way)
+        pass_on(0, 1, way, False)
+    for way in range(2):
+        prepare(1, 0, way)
+        pass_on(1, 0, way, False)
+    for way in range(2):
+        prepare(1, 1, way)
+    for way in range(2):
+        prepare(2, 0, way)
+    for way in range(2):
+        pass_on(1, 1, way, True)
+        prepare(2, 1, way)
 
     def sum_step(s, carry):
         for way in range(2):
-            pass_on(s, 1 - way, way, True)
+            pass_on(s, 0, way, True)
+            prepare(s + 1, 0, way)
         for way in range(2):
-            pass_on(s, way, way, True)
+            pass_on(s, 1, way, True)
+
+            @pl.when(s < 3)
+            def _():
+                prepare(s + 1, 1, way)
         return carry
 
     lax.fori_loop(2, 4, sum_step, 0)
 
     scatter = lambda k: remote(
-        own16.at[(p1 + k) % RING], direct.at[k], l_send.at[k], l_recv.at[k],
+        own16.at[(p1 + k) % RING], direct.at[k], l_send.at[0], l_recv.at[k],
         on_rings((p1 + k) % RING, p2),
     )
     for h in range(2):
-        part = own_part(p2, h)
         halves = []
         for xh in range(2):
             sub = h * 2 + xh
-            value = part[xh * 48:(xh + 1) * 48]
+            value = ahead[1 - h, 0, xh * 48:(xh + 1) * 48, :]
             for way in range(2):
                 sum_copy(way, 3, sub).wait_recv()
                 value = value + came[way, 3, sub].astype(F32)
@@ -304,6 +334,15 @@
             both = jnp.concatenate([v[:, lo * 192:(lo + 1) * 192] for v in halves], axis=1)
             own32[h * 4 + lo] = both
             own16[h * 4 + lo] = both.astype(BF16)
+
+    @pl.when(c == 0)
+    def _():
+        pl.semaphore_signal(pair_sem, inc=1, device_id=sibling, device_id_type=MESH)
+
+    @pl.when(c == 1)
+    def _():
+        pl.semaphore_wait(pair_sem, 1)
+
     for k in (4, 3, 5, 2, 6, 1, 7):
         scatter(k).start()
     total = own32[p1]
@@ -330,6 +369,32 @@
     def _():
         last_in[x] = last_out[x % 2, c]
 
+    for d in (1, 2, 3):
+        table(d).wait_send()
+        remote(
+            tok_ref, near.at[x % 2, c], x_send.at[d], x_recv.at[x % 2, c],
+            device((x + d) % 4, y, z, half),
+        ).wait_send()
+
+    @pl.when(half != c)
+    def _():
+        remote(tok_ref, near.at[x % 2, c], x_send.at[0], x_recv.at[x % 2, c], sibling).wait_send()
+
+    far_table.wait_send()
+    down_copy.wait_send()
+    for k in range(2):
+        mine = wk.at[:, :, pl.ds(pl.multiple_of((2 * k + c) * 128, 128), 128)]
+        pltpu.make_async_copy(mine, mine, w_sem.at[2 + k]).wait()
+
+    for sem, kept in ((f_send, first), (l_send, own16), (a_send, blocks), (r_send, blocks)):
+        gone = kept.at[pl.ds(0, 7)]
+        pltpu.make_async_copy(gone, gone, sem.at[0]).wait()
+    for xt in range(2):
+        for ct in range(2):
+            @pl.when((2 * c + xt != x) | (c != ct))
+            def _():
+                home(xt, ct).wait_send()
+
     for xs in range(4):
         @pl.when((xs != x) | (half != c))
         def _():
@@ -338,49 +403,10 @@
             ).wait_recv()
     out_ref[...] = (last_in[0] + last_in[1] + last_in[2] + last_in[3]).astype(BF16)
 
-    for xt in range(2):
-        for ct in range(2):
-            @pl.when((2 * c + xt != x) | (c != ct))
-            def _():
-                home(xt, ct).wait_send()
-    for k in range(1, RING):
-        scatter(k).wait_send()
-        around(k).wait_send()
-    for d in (1, 2, 3):
-        table(d).wait_send()
-        remote(
-            tok_ref, near.at[x % 2, c], x_send.at[d], x_recv.at[x % 2, c],
-            device((x + d) % 4, y, z, half),
-        ).wait_send()
-
-    @pl.when(half != c)
-    def _():
-        remote(tok_ref, near.at[x % 2, c], x_send.at[0], x_recv.at[x % 2, c], sibling).wait_send()
-
-    far_table.wait_send()
-    down_copy.wait_send()
-    for k in range(2):
-        mine = wk.at[:, :, pl.ds(pl.multiple_of((2 * k + c) * 128, 128), 128)]
-        pltpu.make_async_copy(mine, mine, w_sem.at[2 + k]).wait()
-
-    def left(s, carry):
-        for way in range(2):
-            for sub in range(4):
-                ring_copy(way, s, p2, sub).wait_send()
-                sum_copy(way, s + 1, sub).wait_send()
-        return carry
-
-    lax.fori_loop(0, 3, left, 0)
-    for way in range(2):
-        for xh in range(2):
-            ring_copy(way, 3, p2, way * 2 + xh).wait_send()
-            sum_copy(way, 0, way * 2 + xh).wait_send()
-
-
 def local(tokens, expert_ids, route_weight, gate_weight, up_weight, down_weight):
     vmem, dma = pltpu.VMEM, pltpu.SemaphoreType.DMA
     inside = pl.BlockSpec(memory_space=pltpu.VMEM)
-    outside = pl.BlockSpec(memory_space=pl.ANY)
+    outside = pl.BlockSpec(memory_space=pltpu.HBM)
     return pl.pallas_call(
         kernel,
         name="layer",
@@ -388,20 +414,23 @@
             jax.ShapeDtypeStruct((48, 96), BF16),
             jax.ShapeDtypeStruct((2, 8), F32),
         ),
-        in_specs=[inside] * 3 + [outside] * 3,
+        in_specs=[outside] * 6,
         out_specs=(inside, inside),
         scratch_shapes=[
+            vmem((48, 96), BF16),
+            vmem((2, 48), jnp.int32),
+            vmem((2, 48), jnp.int32),
             vmem((2, 2, 48, 96), BF16),
-            vmem((128, 128), F32),
             vmem((2, 4, 8, 128), F32),
             vmem((8, 48, 384), BF16),
-            vmem((8, 4, 48, 768), BF16),
+            vmem((8, 8, 48, 384), BF16),
             vmem((8, 768, 512), BF16),
             vmem((256, 6144), BF16),
             vmem((8, 256, 768), BF16),
             vmem((2, 96, 512), F32),
             vmem((2, 96, 256), BF16),
             vmem((2, 96, 128), F32),
+            vmem((2, 2, 96, 768), F32),
             vmem((2, 4, 4, 48, 768), BF16),
             vmem((2, 4, 4, 48, 768), BF16),
             vmem((8, 48, 384), F32),
@@ -409,27 +438,32 @@
             vmem((8, 48, 384), BF16),
             vmem((2, 2, 48, 96), F32),
             vmem((4, 48, 96), F32),
+            dma((3,)),
             dma((6,)),
             dma((3,)),
             dma((4,)),
             dma((2, 2)),
             dma((4,)),
             dma((4,)),
+            dma((1,)),
             dma((8,)),
-            dma((8,)),
+            dma((1,)),
+            dma((2, 4, 8)),
+            dma((1,)),
             dma((2, 4, 4)),
-            dma((2, 4, 4)),
-            dma((2, 4, 4)),
-            dma((2, 4, 4)),
-            dma((8,)),
+            dma((1,)),
             dma((8,)),
             dma((2, 2)),
             dma((4,)),
+            pltpu.SemaphoreType.REGULAR,
         ],
         compiler_params=pltpu.CompilerParams(
             collective_id=0, has_side_effects=True, vmem_limit_bytes=48 * 1024 * 1024
         ),
-    )(tokens, expert_ids, route_weight, gate_weight, up_weight, down_weight)
+    )(*[
+        pltpu.with_memory_space_constraint(a, pltpu.HBM)
+        for a in (tokens, expert_ids.T, route_weight.T, gate_weight, up_weight, down_weight)
+    ])
 
 
 def solution(mesh):

time: 85 us -> 72.7 us (0.86)
  local copies, waits for them, and re-layouts: 7.62 us -> 1.16 us
  Pallas kernels: 76.4 us -> 70.8 us
    unnamed x12 -> x2, local copies, waits for them, and re-layouts: 7.62 us -> 1.16 us
    pallas_call x1, Pallas kernels: 76.4 us -> 70.8 us  [local(): pl.pallas_call(kernel, name='layer', out_shape=(jax.ShapeDtypeStruct((48,...]
where the time goes in v2:
time: 72.7 us; the launch traced here: 72.6 us
  Pallas kernels  70.8 us (97%)
  local copies, waits for them, and re-layouts  1.16 us (2%)
    pallas_call x1, Pallas kernels, local(): pl.pallas_call(kernel, name='layer', out_shape=(jax.ShapeDtypeStruct((48,...  70.8 us

profile of v2, /device:TPU:1, one launch (start us, length us, event | category | flops | bytes accessed | tf_op | source)
XLA Modules:
  0.0 72.6 jit_solution(10699587897392192917)
XLA Ops:
  0.6 70.8 %layer.1 = (bf16[48,96]{1,0:T(8,128)(2,1)S(1)}, f32[2,8]{1,0:T(2,128)S(1)}) custom-call(bf16[48,96]{1,0:T(8,128)(2,1)} %tok_hbm.1, s32[2,48]{1,0:T(2,128)} %bitcast.2, s32[2,48]{1,0:T(2,128)} %bitcast.3, bf16[1,6144,128]{2,1,0:T(8,128)(2,1)} %gate_ref.1, bf16[1,6144,128]{2,1,0:T(8,128)(2,1)} %up_ref.1, bf16[1,128,6144]{2,1,0:T(8,128)(2,1)} %down_ref.1), custom_call_target="tpu_custom_call" | custom-call | tf_op jit(solution)/shard_map/layer/pallas_call | solution.py:410
  71.4 0.6 copy.10
  72.0 0.6 copy.11

commit v3 on v2

v3 whole, which is shorter than its diff:
```python
import jax
import jax.numpy as jnp
from jax import lax
from jax.experimental import pallas as pl
from jax.experimental.pallas import tpu as pltpu
from jax.sharding import PartitionSpec as P

MESH = pl.DeviceIdType.MESH
F32 = jnp.float32
BF16 = jnp.bfloat16
RING = 8


def kernel(
    tok_hbm, ids_hbm, raw_hbm, gate_ref, up_ref, down_ref,
    out_ref, load_ref,
    tok_ref, ids_ref, raw_ref, near, tabs, first, blocks, wk, dn, dk, acc, hid, scl, ahead,
    sent, came, own32, own16, direct, last_out, last_in,
    in_sem, w_sem, d_sem, x_send, x_recv, t_send, t_recv, f_send, f_recv,
    a_send, a_recv, r_send, r_recv, l_send, l_recv, o_send, o_recv,
):
    e = lax.axis_index("expert")
    t = lax.axis_index("tensor")
    x, z_hi = e // 2, e % 2
    y, z_lo, c = t // 8, (t // 2) % 4, t % 2
    z = z_hi * 4 + z_lo
    half = x // 2
    role = (c + y + z) % 2
    p1 = z + role * (y - z)
    p2 = y + role * (z - y)

    def device(x_, y_, z_, c_):
        return (x_ * 2 + z_ // 4, (y_ * 4 + z_ % 4) * 2 + c_)

    def on_rings(a, b):
        y_, z_ = b + role * (a - b), a + role * (b - a)
        return device(x, y_, z_, (role + y_ + z_) % 2)

    def remote(src, dst, send, recv, target):
        return pltpu.make_async_remote_copy(
            src_ref=src, dst_ref=dst, send_sem=send, recv_sem=recv,
            device_id=target, device_id_type=MESH,
        )

    sibling = device(x, y, z, 1 - c)

    barrier = pltpu.get_barrier_semaphore()

    def greet(target):
        pl.semaphore_signal(barrier, inc=1, device_id=target, device_id_type=MESH)

    for k in (4, 3, 5, 2, 6, 1, 7):
        other = (x * 2 + c + k) % 8
        greet(on_rings((p1 + k) % RING, p2))
        if k in (1, 4, 7):
            greet(on_rings(p1, (p2 + k) % RING))
        greet(device(other // 2, y, z, other % 2))

    def weight_rows(i, path):
        kb, j = i // 4, i % 4
        straight = kb * 768 + j * 192
        across = ((kb % 2) * 4 + j) * 768 + (kb // 2) * 192
        return pl.ds(pl.multiple_of(straight + path * (across - straight), 64), 192)

    def weight_slot(i, k):
        return wk.at[i // 4, pl.ds(pl.multiple_of((i % 4) * 192, 64), 192), pl.ds(pl.multiple_of(k * 128, 128), 128)]

    def local_weights(i, carry):
        rows = weight_rows(i, role)
        pltpu.make_async_copy(gate_ref.at[0, rows, :], weight_slot(i, c), w_sem.at[0]).start()
        pltpu.make_async_copy(up_ref.at[0, rows, :], weight_slot(i, 2 + c), w_sem.at[1]).start()
        return carry

    tok_copy = pltpu.make_async_copy(tok_hbm, tok_ref, in_sem.at[0])
    ids_copy = pltpu.make_async_copy(ids_hbm, ids_ref, in_sem.at[1])
    raw_copy = pltpu.make_async_copy(raw_hbm, raw_ref, in_sem.at[2])
    tok_copy.start()
    ids_copy.start()
    raw_copy.start()
    own_down = dn.at[pl.ds(pl.multiple_of(c * 128, 128), 128), :]
    their_down = dn.at[pl.ds(pl.multiple_of((1 - c) * 128, 128), 128), :]
    pltpu.make_async_copy(down_ref.at[0], own_down, d_sem.at[0]).start()

    lax.fori_loop(0, 32, local_weights, 0)

    ids_copy.wait()
    raw_copy.wait()
    row = lax.broadcasted_iota(jnp.int32, (8, 48), 0)
    weights = raw_ref[...].astype(F32)
    share = weights / (weights[0:1, :] + weights[1:2, :])
    ids = ids_ref[...]
    zero = jnp.zeros((8, 48), F32)
    hit0 = ids[0:1, :] == row
    hit1 = ids[1:2, :] == row
    mix = jnp.where(hit0, share[0:1, :], zero) + jnp.where(hit1, share[1:2, :], zero)
    hits = jnp.where(hit0, 1.0, zero) + jnp.where(hit1, 1.0, zero)
    tabs[z_hi, x, :, 0:48] = mix
    tabs[z_hi, x, :, 48:128] = jnp.where(
        lax.broadcasted_iota(jnp.int32, (8, 80), 1) == 0,
        jnp.sum(hits, axis=1, keepdims=True), jnp.sum(mix, axis=1, keepdims=True),
    )

    tok_copy.wait()
    pl.semaphore_wait(barrier, 17)

    for d in (2, 1, 3):
        remote(
            tok_ref, near.at[x % 2, c], x_send.at[d], x_recv.at[x % 2, c],
            device((x + d) % 4, y, z, (half + y + z) % 2),
        ).start()

    @pl.when(half != role)
    def _():
        remote(tok_ref, near.at[x % 2, c], x_send.at[0], x_recv.at[x % 2, c], sibling).start()

    @pl.when(half == role)
    def _():
        near[x % 2, c] = tok_ref[...]

    table = lambda d: remote(
        tabs.at[z_hi, x], tabs.at[z_hi, x], t_send.at[d], t_recv.at[d],
        device((x + d) % 4, y, z, c),
    )
    for d in (1, 2, 3):
        table(d).start()

    def remote_weights(i, carry):
        rows = weight_rows(i, 1 - role)
        remote(gate_ref.at[0, rows, :], weight_slot(i, c), w_sem.at[2], w_sem.at[4], sibling).start()
        remote(up_ref.at[0, rows, :], weight_slot(i, 2 + c), w_sem.at[3], w_sem.at[5], sibling).start()
        return carry

    down_copy = remote(down_ref.at[0], own_down, d_sem.at[1], d_sem.at[2], sibling)
    down_copy.start()
    lax.fori_loop(0, 32, remote_weights, 0)

    for xh in range(2):
        for cs in range(2):
            @pl.when((2 * role + xh != x) | (c != cs))
            def _():
                remote(
                    tok_ref, near.at[xh, cs], x_send.at[0], x_recv.at[xh, cs], sibling
                ).wait_recv()

    pieces = [near[xh, cs].astype(F32) for xh in range(2) for cs in range(2)]
    first[p1] = jnp.concatenate(pieces, axis=1).astype(BF16)

    around = lambda k: remote(
        first.at[p1], first.at[p1], f_send.at[0], f_recv.at[k], on_rings((p1 + k) % RING, p2)
    )
    for k in (1, 7, 4, 3, 5, 2, 6):
        around(k).start()
    for d in (1, 2, 3):
        remote(
            tabs.at[z_hi, x], tabs.at[z_hi, (x + 4 - d) % 4], t_send.at[d], t_recv.at[d], sibling
        ).wait_recv()
    mirror = device(x, y, (z + 4) % 8, c)
    far_table = remote(tabs.at[z_hi], tabs.at[z_hi], t_send.at[0], t_recv.at[0], mirror)
    far_table.start()

    acc[...] = jnp.zeros_like(acc)

    pair = p1 // 2
    pairs = [pair, (pair + 1) % 4, (pair + 3) % 4, (pair + 2) % 4]

    def near_first(h, rank):
        same = (pair // 2 + h + 1) % 2
        return (pair % 2 + 1 - same + rank) % 2

    def piece(pr, xh):
        return (pr // 2) * 4 + xh * 2 + pr % 2

    pltpu.make_async_copy(down_ref.at[0], own_down, d_sem.at[0]).wait()
    pltpu.make_async_copy(down_ref.at[0], their_down, d_sem.at[2]).wait()

    @pl.when(role == 0)
    def _():
        for kb in range(8):
            dk[kb] = dn[:, kb * 768:(kb + 1) * 768]

    @pl.when(role == 1)
    def _():
        def repack(g, carry):
            rows = pl.ds(pl.multiple_of(g * 32, 32), 32)
            for kb in range(8):
                lo, hi = kb // 2, kb % 2
                cuts = [
                    dn[rows, (hi * 4 + j) * 768 + lo * 192:(hi * 4 + j) * 768 + (lo + 1) * 192].astype(F32)
                    for j in range(4)
                ]
                dk[kb, rows, :] = jnp.concatenate(cuts, axis=1).astype(BF16)
            return carry

        lax.fori_loop(0, 8, repack, 0)

    def ring_copy(way, step, b, sub):
        target = on_rings(p1, (p2 + (1 if way == 0 else 7)) % RING)
        return remote(
            blocks.at[b, sub], blocks.at[b, sub],
            a_send.at[0], a_recv.at[way, step, sub], target,
        )

    def first_come(source):
        k = (p1 + RING - source) % RING
        remote(first.at[p1], first.at[source], f_send.at[0], f_recv.at[k], sibling).wait_recv()

    for j in range(4):
        if j == 0:
            first_come(p1 + 1 - 2 * (p1 % 2))
        else:
            first_come(pairs[j] * 2)
            first_come(pairs[j] * 2 + 1)
        for xh in range(2):
            sub = piece(pairs[j], xh)
            parts = [
                first[pairs[j] * 2 + lo][:, xh * 192:(xh + 1) * 192].astype(F32) for lo in range(2)
            ]
            blocks[p2, sub] = jnp.concatenate(parts, axis=1).astype(BF16)
            ring_copy(0, 0, p2, sub).start()
            ring_copy(1, 0, p2, sub).start()

    def place(b, h):
        across = (b % 4) * 2 + h
        return b + role * (across - b), h + role * (b // 4 - h)

    def project(b, h):
        kb, r = place(b, h)
        part = blocks[b, pl.ds(4 * h, 4)]
        rows = jnp.concatenate(
            [jnp.concatenate([part[2 * xh], part[2 * xh + 1]], axis=1) for xh in range(2)], axis=0
        )
        acc[r] += jnp.dot(rows, wk[kb], preferred_element_type=F32)

    def weights_here():
        for k in range(2):
            mine = wk.at[:, :, pl.ds(pl.multiple_of((2 * k + c) * 128, 128), 128)]
            theirs = wk.at[:, :, pl.ds(pl.multiple_of((2 * k + 1 - c) * 128, 128), 128)]
            pltpu.make_async_copy(mine, mine, w_sem.at[k]).wait()
            pltpu.make_async_copy(theirs, theirs, w_sem.at[4 + k]).wait()

    def gather_step(r, carry):
        held = ((p2 + RING - r) % RING, (p2 + r) % RING)
        before = ((p2 + RING + 1 - r) % RING, (p2 + r - 1) % RING)
        for j in range(4):
            h = pairs[j] // 2
            for xh in range(2):
                sub = piece(pairs[j], xh)
                for way in range(2):
                    ring_copy(way, r - 1, held[way], sub).wait_recv()

                    @pl.when((r < 3) | (h == way))
                    def _():
                        ring_copy(way, r, held[way], sub).start()

                if xh == 0 and j == 0:
                    pl.when(r == 1)(weights_here)
                if xh == 0 and j % 2 == 0:
                    project(before[0], j // 2)
                elif xh == 0:
                    @pl.when(r > 1)
                    def _():
                        project(before[1], j // 2)
        return carry

    lax.fori_loop(1, 4, gather_step, 0)
    far = (p2 + 4) % RING
    for rank in range(2):
        for xh in range(2):
            for way in range(2):
                sub = way * 4 + xh * 2 + near_first(way, rank)
                ring_copy(way, 3, far, sub).wait_recv()
            project((p2 + (5 if xh == 0 else 3)) % RING, rank)
    for way in range(2):
        project(far, way)

    remote(tabs.at[z_hi], tabs.at[1 - z_hi], t_send.at[0], t_recv.at[0], mirror).wait_recv()
    lane96 = lax.broadcasted_iota(jnp.int32, (128, 8), 1)
    for r in range(2):
        for xh in range(2):
            turned = jnp.transpose(tabs[r, 2 * role + xh])
            picked = jnp.sum(jnp.where(lane96 == e, turned, 0.0), axis=1, keepdims=True)
            scl[r, xh * 48:(xh + 1) * 48, :] = jnp.broadcast_to(picked[0:48], (48, 128))
        gate = acc[r, :, 0:256]
        up = acc[r, :, 256:512]
        hid[r] = (gate / (1.0 + jnp.exp(-gate)) * up).astype(BF16)
    everyone = tabs[0, 0]
    for k in range(1, 8):
        everyone = everyone + tabs[k // 4, k % 4]
    load_ref[...] = jnp.transpose(everyone)[48:50, :] / 48.0

    def own_part(q, h):
        kb, r = place(q, h)
        part = jnp.dot(hid[r], dk[kb], preferred_element_type=F32)
        return part * scl[r][:, 0:1]

    def sum_copy(way, s, sub):
        target = on_rings(p1, (p2 + (1 if way == 0 else 7)) % RING)
        return remote(
            sent.at[way, s, sub], came.at[way, s, sub],
            r_send.at[0], r_recv.at[way, s, sub], target,
        )

    def prepare(s, k, way):
        q = (p2 + (4 - s if way == 0 else 4 + s)) % RING
        part = own_part(q, 1 - way if k == 0 else way)
        for xh in range(2):
            for lh in range(2):
                ahead[way, k, xh, lh] = part[xh * 48:(xh + 1) * 48, lh * 384:(lh + 1) * 384]

    def pass_on(s, k, has_come, following=None):
        for i in range(4):
            xh = i % 2
            for way in range(2):
                h = 1 - way if k == 0 else way
                lh = near_first(h, 1 - i // 2)
                sub = h * 4 + xh * 2 + lh
                value = ahead[way, k, xh, lh]
                if has_come:
                    sum_copy(way, s - 1, sub).wait_recv()
                    value = value + came[way, s - 1, sub].astype(F32)
                sent[way, s, sub] = value.astype(BF16)
                sum_copy(way, s, sub).start()
            if following is not None and i % 2 == 0:
                prepare(*following, i // 2)

    for way in range(2):
        prepare(0, 1, way)
    pass_on(0, 1, False, (1, 0))
    pass_on(1, 0, False)
    for way in range(2):
        prepare(1, 1, way)
    pass_on(1, 1, True, (2, 0))

    def sum_step(s, carry):
        pass_on(s, 0, True, (s, 1))
        pass_on(s, 1, True, (s + 1, 0))
        return carry

    lax.fori_loop(2, 4, sum_step, 0)

    def scatter(target):
        k = (target + RING - p1) % RING
        return remote(
            own16.at[target], direct.at[k], l_send.at[0], l_recv.at[k], on_rings(target, p2)
        )

    def scatter_pair(pr):
        for lo in range(2):
            target = pr * 2 + lo

            @pl.when(target != p1)
            def _():
                scatter(target).start()

    for rank in (1, 0):
        for h in range(2):
            lh = near_first(h, rank)
            halves = []
            for xh in range(2):
                sub = h * 4 + xh * 2 + lh
                value = ahead[1 - h, 0, xh, lh]
                for way in (1 - h, h):
                    sum_copy(way, 3, sub).wait_recv()
                    value = value + came[way, 3, sub].astype(F32)
                halves.append(value)
            for lo in range(2):
                both = jnp.concatenate([v[:, lo * 192:(lo + 1) * 192] for v in halves], axis=1)
                own32[h * 4 + lh * 2 + lo] = both
                own16[h * 4 + lh * 2 + lo] = both.astype(BF16)

            scatter_pair(h * 2 + lh)

    for d in (1, 2, 3):
        table(d).wait_send()
        remote(
            tok_ref, near.at[x % 2, c], x_send.at[d], x_recv.at[x % 2, c],
            device((x + d) % 4, y, z, (half + y + z) % 2),
        ).wait_send()

    @pl.when(half != role)
    def _():
        remote(tok_ref, near.at[x % 2, c], x_send.at[0], x_recv.at[x % 2, c], sibling).wait_send()

    far_table.wait_send()
    down_copy.wait_send()
    for k in range(2):
        mine = wk.at[:, :, pl.ds(pl.multiple_of((2 * k + c) * 128, 128), 128)]
        pltpu.make_async_copy(mine, mine, w_sem.at[2 + k]).wait()

    for sem, kept in ((f_send, first), (a_send, blocks), (r_send, blocks)):
        gone = kept.at[pl.ds(0, 7)]
        pltpu.make_async_copy(gone, gone, sem.at[0]).wait()
    total = own32[p1]
    for k in (1, 7, 2, 6, 3, 5, 4):
        remote(own16.at[0], direct.at[k], l_send.at[0], l_recv.at[k], sibling).wait_recv()
        total = total + direct[k].astype(F32)
    for xt in range(2):
        for ct in range(2):
            last_out[xt, ct] = total[:, xt * 192 + ct * 96:xt * 192 + (ct + 1) * 96]

    def home(xt, ct):
        return remote(
            last_out.at[xt, ct], last_in.at[x], o_send.at[xt, ct], o_recv.at[x],
            device(2 * role + xt, y, z, ct),
        )

    for xt in range(2):
        for ct in range(2):
            @pl.when((2 * role + xt != x) | (c != ct))
            def _():
                home(xt, ct).start()

    @pl.when(half == role)
    def _():
        last_in[x] = last_out[x % 2, c]

    for xs in range(4):
        @pl.when((xs != x) | (half != role))
        def _():
            remote(
                last_out.at[0, 0], last_in.at[xs], o_send.at[0, 0], o_recv.at[xs], sibling
            ).wait_recv()
    out_ref[...] = (last_in[0] + last_in[1] + last_in[2] + last_in[3]).astype(BF16)
    for xt in range(2):
        for ct in range(2):
            @pl.when((2 * role + xt != x) | (c != ct))
            def _():
                home(xt, ct).wait_send()
    gone = own16.at[pl.ds(0, 7)]
    pltpu.make_async_copy(gone, gone, l_send.at[0]).wait()


def local(tokens, expert_ids, route_weight, gate_weight, up_weight, down_weight):
    vmem, dma = pltpu.VMEM, pltpu.SemaphoreType.DMA
    inside = pl.BlockSpec(memory_space=pltpu.VMEM)
    outside = pl.BlockSpec(memory_space=pltpu.HBM)
    return pl.pallas_call(
        kernel,
        name="layer",
        out_shape=(
            jax.ShapeDtypeStruct((48, 96), BF16),
            jax.ShapeDtypeStruct((2, 8), F32),
        ),
        in_specs=[outside] * 6,
        out_specs=(inside, inside),
        scratch_shapes=[
            vmem((48, 96), BF16),
            vmem((2, 48), jnp.int32),
            vmem((2, 48), jnp.int32),
            vmem((2, 2, 48, 96), BF16),
            vmem((2, 4, 8, 128), F32),
            vmem((8, 48, 384), BF16),
            vmem((8, 8, 48, 384), BF16),
            vmem((8, 768, 512), BF16),
            vmem((256, 6144), BF16),
            vmem((8, 256, 768), BF16),
            vmem((2, 96, 512), F32),
            vmem((2, 96, 256), BF16),
            vmem((2, 96, 128), F32),
            vmem((2, 2, 2, 2, 48, 384), F32),
            vmem((2, 4, 8, 48, 384), BF16),
            vmem((2, 4, 8, 48, 384), BF16),
            vmem((8, 48, 384), F32),
            vmem((8, 48, 384), BF16),
            vmem((8, 48, 384), BF16),
            vmem((2, 2, 48, 96), F32),
            vmem((4, 48, 96), F32),
            dma((3,)),
            dma((6,)),
            dma((3,)),
            dma((4,)),
            dma((2, 2)),
            dma((4,)),
            dma((4,)),
            dma((1,)),
            dma((8,)),
            dma((1,)),
            dma((2, 4, 8)),
            dma((1,)),
            dma((2, 4, 8)),
            dma((1,)),
            dma((8,)),
            dma((2, 2)),
            dma((4,)),
        ],
        compiler_params=pltpu.CompilerParams(
            collective_id=0, has_side_effects=True, vmem_limit_bytes=48 * 1024 * 1024
        ),
    )(*[
        pltpu.with_memory_space_constraint(a, pltpu.HBM)
        for a in (tokens, expert_ids.T, route_weight.T, gate_weight, up_weight, down_weight)
    ])


def solution(mesh):
    placed = (
        P("expert", "tensor"),
        P("expert", None),
        P("expert", None),
        P("expert", None, "tensor"),
        P("expert", None, "tensor"),
        P("expert", "tensor", None),
    )
    return jax.shard_map(
        local, mesh=mesh, in_specs=placed, out_specs=(P("expert", "tensor"), P()), check_vma=False
    )
```

time: 72.7 us -> 68.3 us (0.939); the launches traced: 72.6 us -> 67 us
  Pallas kernels: 70.8 us -> 65.2 us
    pallas_call x1, Pallas kernels: 70.8 us -> 65.2 us  [local(): pl.pallas_call(kernel, name='layer', out_shape=(jax.ShapeDtypeStruct((48,...]
where the time goes in v3:
time: 68.3 us; the launch traced here: 67 us
  Pallas kernels  65.2 us (95%)
  local copies, waits for them, and re-layouts  1.16 us (2%)
    pallas_call x1, Pallas kernels, local(): pl.pallas_call(kernel, name='layer', out_shape=(jax.ShapeDtypeStruct((48,...  65.2 us

profile of v3, /device:TPU:1, one launch (start us, length us, event | category | flops | bytes accessed | tf_op | source)
XLA Modules:
  0.0 67.0 jit_solution(12813435678897811002)
XLA Ops:
  0.6 65.2 %layer.1 = (bf16[48,96]{1,0:T(8,128)(2,1)S(1)}, f32[2,8]{1,0:T(2,128)S(1)}) custom-call(bf16[48,96]{1,0:T(8,128)(2,1)} %tok_hbm.1, s32[2,48]{1,0:T(2,128)} %bitcast.2, s32[2,48]{1,0:T(2,128)} %bitcast.3, bf16[1,6144,128]{2,1,0:T(8,128)(2,1)} %gate_ref.1, bf16[1,6144,128]{2,1,0:T(8,128)(2,1)} %up_ref.1, bf16[1,128,6144]{2,1,0:T(8,128)(2,1)} %down_ref.1), custom_call_target="tpu_custom_call" | custom-call | tf_op jit(solution)/shard_map/layer/pallas_call | solution.py:437
  65.8 0.6 copy.10
  66.4 0.6 copy.11

commit v4 on v3

--- a/solution.py
+++ b/solution.py
@@ -148,7 +148,7 @@
     around = lambda k: remote(
         first.at[p1], first.at[p1], f_send.at[0], f_recv.at[k], on_rings((p1 + k) % RING, p2)
     )
-    for k in (1, 7, 4, 3, 5, 2, 6):
+    for k in (4, 3, 5, 2, 6, 1, 7):
         around(k).start()
     for d in (1, 2, 3):
         remote(
@@ -197,7 +197,7 @@
         target = on_rings(p1, (p2 + (1 if way == 0 else 7)) % RING)
         return remote(
             blocks.at[b, sub], blocks.at[b, sub],
-            a_send.at[0], a_recv.at[way, step, sub], target,
+            a_send.at[0], a_recv.at[way, step * 8 + sub - step // 3 * way * 4], target,
         )
 
     def first_come(source):
@@ -263,6 +263,18 @@
         return carry
 
     lax.fori_loop(1, 4, gather_step, 0)
+    remote(tabs.at[z_hi], tabs.at[1 - z_hi], t_send.at[0], t_recv.at[0], mirror).wait_recv()
+    lane96 = lax.broadcasted_iota(jnp.int32, (128, 8), 1)
+    for r in range(2):
+        for xh in range(2):
+            turned = jnp.transpose(tabs[r, 2 * role + xh])
+            picked = jnp.sum(jnp.where(lane96 == e, turned, 0.0), axis=1, keepdims=True)
+            scl[r, xh * 48:(xh + 1) * 48, :] = jnp.broadcast_to(picked[0:48], (48, 128))
+    everyone = tabs[0, 0]
+    for k in range(1, 8):
+        everyone = everyone + tabs[k // 4, k % 4]
+    load_ref[...] = jnp.transpose(everyone)[48:50, :] / 48.0
+
     far = (p2 + 4) % RING
     for rank in range(2):
         for xh in range(2):
@@ -273,20 +285,10 @@
     for way in range(2):
         project(far, way)
 
-    remote(tabs.at[z_hi], tabs.at[1 - z_hi], t_send.at[0], t_recv.at[0], mirror).wait_recv()
-    lane96 = lax.broadcasted_iota(jnp.int32, (128, 8), 1)
     for r in range(2):
-        for xh in range(2):
-            turned = jnp.transpose(tabs[r, 2 * role + xh])
-            picked = jnp.sum(jnp.where(lane96 == e, turned, 0.0), axis=1, keepdims=True)
-            scl[r, xh * 48:(xh + 1) * 48, :] = jnp.broadcast_to(picked[0:48], (48, 128))
         gate = acc[r, :, 0:256]
         up = acc[r, :, 256:512]
         hid[r] = (gate / (1.0 + jnp.exp(-gate)) * up).astype(BF16)
-    everyone = tabs[0, 0]
-    for k in range(1, 8):
-        everyone = everyone + tabs[k // 4, k % 4]
-    load_ref[...] = jnp.transpose(everyone)[48:50, :] / 48.0
 
     def own_part(q, h):
         kb, r = place(q, h)
@@ -297,7 +299,7 @@
         target = on_rings(p1, (p2 + (1 if way == 0 else 7)) % RING)
         return remote(
             sent.at[way, s, sub], came.at[way, s, sub],
-            r_send.at[0], r_recv.at[way, s, sub], target,
+            r_send.at[0], r_recv.at[way, (s * 8 + sub - 4) if s is not None and not isinstance(s, int) else (sub - way * 4 if s == 0 else s * 8 + sub - 4)], target,
         )
 
     def prepare(s, k, way):
@@ -430,11 +432,23 @@
     pltpu.make_async_copy(gone, gone, l_send.at[0]).wait()
 
 
+def hand_out(mixed_ref, load_ref, mixed_out, load_out, sem):
+    copies = [
+        pltpu.make_async_copy(mixed_ref, mixed_out, sem.at[0]),
+        pltpu.make_async_copy(load_ref, load_out, sem.at[1]),
+    ]
+    for copy in copies:
+        copy.start()
+    for copy in copies:
+        copy.wait()
+
+
 def local(tokens, expert_ids, route_weight, gate_weight, up_weight, down_weight):
     vmem, dma = pltpu.VMEM, pltpu.SemaphoreType.DMA
     inside = pl.BlockSpec(memory_space=pltpu.VMEM)
     outside = pl.BlockSpec(memory_space=pltpu.HBM)
-    return pl.pallas_call(
+    shapes = (jax.ShapeDtypeStruct((48, 96), BF16), jax.ShapeDtypeStruct((2, 8), F32))
+    result = pl.pallas_call(
         kernel,
         name="layer",
         out_shape=(
@@ -475,9 +489,9 @@
             dma((1,)),
             dma((8,)),
             dma((1,)),
-            dma((2, 4, 8)),
+            dma((2, 28)),
             dma((1,)),
-            dma((2, 4, 8)),
+            dma((2, 28)),
             dma((1,)),
             dma((8,)),
             dma((2, 2)),
@@ -490,6 +504,15 @@
         pltpu.with_memory_space_constraint(a, pltpu.HBM)
         for a in (tokens, expert_ids.T, route_weight.T, gate_weight, up_weight, down_weight)
     ])
+    return pl.pallas_call(
+        hand_out,
+        name="hand_out",
+        out_shape=shapes,
+        in_specs=[inside] * 2,
+        out_specs=(outside, outside),
+        scratch_shapes=[dma((2,))],
+        compiler_params=pltpu.CompilerParams(vmem_limit_bytes=1024 * 1024),
+    )(*result)
 
 
 def solution(mesh):

time: 68.3 us -> 66.1 us (0.968)
  local copies, waits for them, and re-layouts: 1.16 us -> 0 us
    unnamed x2 -> x0, local copies, waits for them, and re-layouts: 1.16 us -> none
    pallas_call x1, Pallas kernels: 65.2 us -> 64.1 us  [local(): pl.pallas_call(kernel, name='layer', out_shape=(jax.ShapeDtypeStruct((48,...]
where the time goes in v4:
time: 66.1 us; the launch traced here: 65.4 us
  Pallas kernels  64.8 us (98%)
    pallas_call x1, Pallas kernels, local(): pl.pallas_call(kernel, name='layer', out_shape=(jax.ShapeDtypeStruct((48,...  64.1 us

profile of v4, /device:TPU:1, one launch (start us, length us, event | category | flops | bytes accessed | tf_op | source)
XLA Modules:
  0.0 65.4 jit_solution(7313932642208667187)
XLA Ops:
  0.6 64.1 %layer.1 = (bf16[48,96]{1,0:T(8,128)(2,1)S(1)}, f32[2,8]{1,0:T(2,128)S(1)}) custom-call(bf16[48,96]{1,0:T(8,128)(2,1)} %tok_hbm.1, s32[2,48]{1,0:T(2,128)} %bitcast.2, s32[2,48]{1,0:T(2,128)} %bitcast.3, bf16[1,6144,128]{2,1,0:T(8,128)(2,1)} %gate_ref.1, bf16[1,6144,128]{2,1,0:T(8,128)(2,1)} %up_ref.1, bf16[1,128,6144]{2,1,0:T(8,128)(2,1)} %down_ref.1), custom_call_target="tpu_custom_call" | custom-call | tf_op jit(solution)/shard_map/layer/pallas_call | solution.py:451
  64.8 0.6 hand_out.1

commit v5 on v4

--- a/solution.py
+++ b/solution.py
@@ -406,8 +406,10 @@
             device(2 * role + xt, y, z, ct),
         )
 
-    for xt in range(2):
+    for rank in range(2):
         for ct in range(2):
+            xt = (x + rank) % 2
+
             @pl.when((2 * role + xt != x) | (c != ct))
             def _():
                 home(xt, ct).start()

time: 66.1 us -> 66.1 us (level)
  no operation moved by 1% of the time
where the time goes in v5:
time: 66.1 us; the launch traced here: 65.4 us
  Pallas kernels  64.8 us (98%)
    pallas_call x1, Pallas kernels, local(): pl.pallas_call(kernel, name='layer', out_shape=(jax.ShapeDtypeStruct((48,...  64.1 us

profile of v5, /device:TPU:1, one launch (start us, length us, event | category | flops | bytes accessed | tf_op | source)
XLA Modules:
  0.0 65.4 jit_solution(3302910909535320754)
XLA Ops:
  0.6 64.1 %layer.1 = (bf16[48,96]{1,0:T(8,128)(2,1)S(1)}, f32[2,8]{1,0:T(2,128)S(1)}) custom-call(bf16[48,96]{1,0:T(8,128)(2,1)} %tok_hbm.1, s32[2,48]{1,0:T(2,128)} %bitcast.2, s32[2,48]{1,0:T(2,128)} %bitcast.3, bf16[1,6144,128]{2,1,0:T(8,128)(2,1)} %gate_ref.1, bf16[1,6144,128]{2,1,0:T(8,128)(2,1)} %up_ref.1, bf16[1,128,6144]{2,1,0:T(8,128)(2,1)} %down_ref.1), custom_call_target="tpu_custom_call" | custom-call | tf_op jit(solution)/shard_map/layer/pallas_call | solution.py:453
  64.8 0.6 hand_out.1
